TPU v7x, 32 devices: a whole 2x2x4 slice. The times are simulated.
32 devices in a mesh: tissue: 2 (over core), row: 4 (over y, x), col: 4 (over z).
Axes of the slice: x: 2, y: 2, z: 4, core: 2. Of those that a mesh axis runs over, the one named last changes fastest.
Arguments:
- expr: float32 [1200, 16384], P(('tissue', 'row'), 'col'), parts along dimension 0, may hold values from -48 to 88
- win_genes: int32 [256], replicated, may hold values from 0 to 16383, as said below
Outputs:
- margin: float32 [512, 16384], P(('tissue', 'row'), 'col'), parts along dimension 0
- degree: float32 [32768], P(('tissue', 'col')), parts along dimension 0
There are 2 independent parts, one for each index of `tissue`. A program takes and returns all parts, laid end to end along the dimension named above; an argument that names none is the same for every part. Nothing has to cross between parts.
Inputs may be any that keep to these rules, and one draw needn't show every extreme that they name: `win_genes`: 256 distinct gene numbers.
All inputs are finite; a program needn't handle non-finite values.
Results may differ from a plain program's by a relative error of at most 0.00077.
Values may be sent and summed in bfloat16 or wider, within the bound.
A program may use at most 128 MiB of HBM per device.

v0:
```python
import jax
import jax.numpy as jnp
from jax import lax
from jax.sharding import PartitionSpec as P


def power_eight(corr):
    half = (1.0 + corr) * 0.5
    half = half * half
    half = half * half
    return half * half


def inner_first(left, right):
    return lax.dot_general(
        left, right, (((0,), (0,)), ((), ())), preferred_element_type=jnp.float32
    )


def body(expr, win_genes):
    n_row = lax.axis_size("row")
    samples_all = expr.shape[0] * n_row
    totals = lax.psum(jnp.sum(expr, axis=0), "row")
    centered = expr - totals / samples_all
    squares = lax.psum(jnp.sum(centered * centered, axis=0), "row")
    z = (centered / jnp.sqrt(squares + 1e-06)).astype(jnp.bfloat16)
    zcol = lax.all_gather(z, "row", axis=0, tiled=True)
    width = zcol.shape[1]
    slab = width // n_row
    row_id = lax.axis_index("row")
    col_id = lax.axis_index("col")
    zpiece = lax.dynamic_slice_in_dim(zcol, row_id * slab, slab, 1)
    zrows = lax.all_gather(zpiece, "col", axis=1, tiled=True)
    adj = power_eight(inner_first(zrows, zcol)).astype(jnp.bfloat16)
    local_rows = jnp.arange(zrows.shape[1], dtype=jnp.int32)
    genes_i = local_rows // slab * width + row_id * slab + local_rows % slab
    genes_j = col_id * width + jnp.arange(width, dtype=jnp.int32)
    keep = genes_i[:, None] != genes_j[None, :]
    partial_degree = jnp.sum(jnp.where(keep, adj.astype(jnp.float32), jnp.float32(0.0)), axis=0)
    degree = lax.psum(partial_degree, "row")
    offsets = win_genes - col_id * width
    inside = (offsets >= 0) & (offsets < width)
    clipped = jnp.clip(offsets, 0, width - 1)
    picked = jnp.take(zcol, clipped, axis=1)
    terms = jnp.where(inside[None, :], picked, jnp.zeros((), jnp.bfloat16))
    zwin = lax.psum(terms, "col").astype(jnp.float32).astype(jnp.bfloat16)
    panel = power_eight(inner_first(zrows, zwin)).astype(jnp.bfloat16)
    margin = lax.psum_scatter(inner_first(panel, adj), "row", scatter_dimension=0, tiled=True)
    return (margin, degree)


def solution(mesh):
    in_specs = (P(("tissue", "row"), "col"), P())
    out_specs = (P(("tissue", "row"), "col"), P(("tissue", "col")))
    return jax.shard_map(body, mesh=mesh, in_specs=in_specs, out_specs=out_specs, check_vma=False)
```

profile of v0, /device:TPU:0, one launch (start us, length us, event | category | flops | bytes accessed | tf_op | source)
XLA Modules:
  0.0 335.1 jit_solution(13726724207227180818)
XLA Ops:
  7.2 0.0 copy-start
  7.2 0.0 all-gather.6.cloned.1.call-start
  7.2 2.0 reduce_sum.27
  9.2 17.5 %psum.28 = f32[4096]{0:T(1024)S(1)} all-reduce(f32[4096]{0:T(1024)S(1)} %reduce_sum.27), channel_id=1, replica_groups=mesh['tissue'=2,'row'=4,'col'=4] {'row'}, use_global_device_ids=true, to_apply=%region_1.0 | all-reduce | flops 4096 | bytes 32768 | tf_op jit(solution)/shard_map/psum | solution.py:23
  26.7 2.0 multiply_reduce_fusion
  28.7 13.7 %psum.29 = f32[4096]{0:T(1024)S(1)} all-reduce(f32[4096]{0:T(1024)S(1)} %multiply_reduce_fusion), channel_id=1, replica_groups=mesh['tissue'=2,'row'=4,'col'=4] {'row'}, use_global_device_ids=true, to_apply=%region_3.0 | all-reduce | flops 4096 | bytes 32768 | tf_op jit(solution)/shard_map/psum | solution.py:25
  42.5 0.0 copy-done
  42.5 1.3 fusion.5
  43.8 0.0 all-gather.6.cloned.1.call-update
  43.8 0.0 all-gather.4.cloned.1.call-start
  43.9 0.0 copy-start.1
  43.9 59.8 %all-gather.6.cloned.1.call-done = bf16[4,150,4096]{2,1,0:T(8,128)(2,1)} async-done(((bf16[1,150,4096]{2,1,0:T(8,128)(2,1)}), bf16[4,150,4096]{2,1,0:T(8,128)(2,1)}) %all-gather.6.cloned.1.call-update) | async-done | bytes 4915216 | tf_op jit(solution)/shard_map/all_gather | solution.py:27
  103.7 6.0 %reshape.49 = bf16[600,4096]{1,0:T(8,128)(2,1)} reshape(bf16[4,150,4096]{2,1,0:T(8,128)(2,1)} %all-gather.6.cloned.1.call-done) | data formatting | bytes 9830400
  109.7 2.4 constant_dynamic-slice_fusion
  112.1 0.0 all-gather.4.cloned.1.call-update
  112.2 0.0 all-reduce.2.cloned.1.call-start
  112.2 0.0 copy-done.1
  112.3 7.9 %copy.6 = bf16[600,4096]{0,1:T(8,128)(2,1)} copy(bf16[600,4096]{1,0:T(8,128)(2,1)} %reshape.49) | data formatting | bytes 9830400
  120.1 4.9 %gather_fusion = bf16[256,600]{1,0:T(8,128)(2,1)S(1)} fusion(bf16[600,4096]{0,1:T(8,128)(2,1)} %copy.6, s32[1024]{0:T(1024)S(1)} %pad_clamp_fusion), kind=kCustom, calls=%fused_computation | custom fusion | bytes 615424 | tf_op jit(solution)/shard_map/jit(_take)/gather | solution.py:44
  125.0 0.9 select_bitcast_fusion
  125.9 0.0 all-reduce.2.cloned.1.call-update
  125.9 0.2 reduce-scatter.2.cloned.1.call-start
  126.1 78.8 %all-gather.4.cloned.1.call-done = bf16[600,4096]{1,0:T(8,128)(2,1)} async-done(((bf16[600,1024]{1,0:T(8,128)(2,1)}), bf16[600,4096]{1,0:T(8,128)(2,1)}) %all-gather.4.cloned.1.call-update) | async-done | bytes 4915216 | tf_op jit(solution)/shard_map/all_gather | solution.py:33
  204.9 45.1 %select_reduce_fusion = (f32[4096]{0:T(1024)S(1)}, bf16[4096,4096]{1,0:T(8,128)(2,1)}) fusion(s32[4096]{0:T(1024)S(1)} %get-tuple-element.8, s32[4096]{0:T(1024)S(1)} %get-tuple-element.7, bf16[600,4096]{1,0:T(8,128)(2,1)} %all-gather.4.cloned.1.call-done, bf16[600,4096]{1,0:T(8,128)(2,1)} %reshape.49), kind=kOutput, calls=%fused_computation.1 | convolution fusion | flops 20300427264 | bytes 43433984 | tf_op jit(solution)/shard_map/dot_general | solution.py:15
  250.1 0.0 all-reduce.2.cloned.1.call-done
  250.1 27.1 %fusion.6 = f32[256,4096]{1,0:T(8,128)} fusion(bf16[4096,4096]{1,0:T(8,128)(2,1)} %get-tuple-element.6, bf16[600,4096]{1,0:T(8,128)(2,1)} %all-gather.4.cloned.1.call-done, bf16[600,256]{0,1:T(8,128)(2,1)} %all-reduce.2.cloned.1.call-done), kind=kOutput, calls=%fused_computation.12 | convolution fusion | flops 9854517248 | bytes 42971136 | tf_op jit(solution)/shard_map/dot_general | solution.py:15
  277.2 0.0 reduce-scatter.2.cloned.1.call-update
  277.2 17.3 %psum.31 = f32[4096]{0:T(1024)} all-reduce(f32[4096]{0:T(1024)S(1)} %get-tuple-element.5), channel_id=1, replica_groups=mesh['tissue'=2,'row'=4,'col'=4] {'row'}, use_global_device_ids=true, to_apply=%region_7.8 | all-reduce | flops 4096 | bytes 32768 | tf_op jit(solution)/shard_map/psum | solution.py:40
  294.5 34.0 %reduce-scatter.2.cloned.1.call-done = f32[64,4096]{1,0:T(8,128)} async-done(((f32[256,4096]{1,0:T(8,128)}), f32[64,4096]{1,0:T(8,128)}) %reduce-scatter.2.cloned.1.call-update) | async-done | bytes 1048592 | tf_op jit(solution)/shard_map/reduce_scatter | solution.py:48
  (5 shorter events, 0.1 us)
Async XLA Ops:
  7.2 35.3 %copy-start = (f32[150,4096]{1,0:T(8,128)S(1)}, f32[150,4096]{1,0:T(8,128)}, u32[]{:S(2)}) copy-start(f32[150,4096]{1,0:T(8,128)} %param.2) | copy-start | bytes 7372804
  7.2 96.5 %all-gather.6.cloned.1.call-start = ((), (), s32[]{:S(2)}) async-start(), calls=%async_computation.4 | async-start | bytes 6225920 | tf_op jit(solution)/shard_map/all_gather | solution.py:27
  43.8 161.1 %all-gather.4.cloned.1.call-start = ((), (), s32[]{:S(2)}) async-start(), calls=%async_computation.1 | async-start | bytes 6144000 | tf_op jit(solution)/shard_map/all_gather | solution.py:33
  43.9 68.3 %copy-start.1 = (s32[256]{0:T(256)S(1)}, s32[256]{0:T(256)}, u32[]{:S(2)}) copy-start(s32[256]{0:T(256)} %param.3) | copy-start | bytes 3076
  112.2 137.9 %all-reduce.2.cloned.1.call-start = ((), (), s32[]{:S(2)}) async-start(), calls=%async_computation.2 | async-start | bytes 655360 | tf_op jit(solution)/shard_map/psum | solution.py:46
  125.9 202.6 %reduce-scatter.2.cloned.1.call-start = ((), (), s32[]{:S(2)}) async-start(), calls=%async_computation.3 | async-start | bytes 5242880 | tf_op jit(solution)/shard_map/reduce_scatter | solution.py:48
Sparse Core Ops, SparseCore 0:
  44.0 59.7 all-gather.5
  112.3 92.6 all-gather.3
  207.9 34.8 all-reduce.1
  277.3 51.1 reduce-scatter.1
where the time goes:
time: 336 us; the launch traced here: 335 us
  waiting for transfers between devices  173 us (51%)
  matrix products  72.2 us (21%)
  blocking collectives  48.5 us (14%)
  local copies, waits for them, and re-layouts  21.1 us (6%)
  between operations  13.8 us (4%)
  other arithmetic  6.23 us (2%)
    all_gather x1, waiting for transfers between devices, body(): zrows = lax.all_gather(zpiece, 'col', axis=1, tiled=True)  78.8 us
    dot_general x2, matrix products, inner_first(): lax.dot_general(left, right, (((0,), (0,)), ((), ())), preferred_element_...  72.2 us
    all_gather x1, waiting for transfers between devices, body(): zcol = lax.all_gather(z, 'row', axis=0, tiled=True)  59.8 us
    reduce_scatter x1, waiting for transfers between devices, body(): lax.psum_scatter(inner_first(panel, adj), 'row', scatter_dimension=0, til...  34 us
    psum x1, blocking collectives, body(): totals = lax.psum(jnp.sum(expr, axis=0), 'row')  17.5 us
    psum x1, blocking collectives, body(): degree = lax.psum(partial_degree, 'row')  17.3 us
    unnamed x6, local copies, waits for them, and re-layouts  13.8 us
    psum x1, blocking collectives, body(): squares = lax.psum(jnp.sum(centered * centered, axis=0), 'row')  13.7 us
  transfers between devices with their start and end apart: 4, of which 3 were waited for; matrix products, arithmetic and copies ran while one was open for 18% of the time, Pallas kernels for 0%

commit v1 on v0

--- a/solution.py
+++ b/solution.py
@@ -2,6 +2,16 @@
 import jax.numpy as jnp
 from jax import lax
 from jax.sharding import PartitionSpec as P
+
+
+def around_the_ring(x, axis, dim):
+    n_dev = lax.axis_size(axis)
+    moving, shards = (x, [x])
+    for _ in range(n_dev - 1):
+        moving = lax.ppermute(moving, axis, [(i, (i + 1) % n_dev) for i in range(n_dev)])
+        shards.insert(0, moving)
+    merged = jnp.concatenate(shards, axis=dim)
+    return jnp.roll(merged, (lax.axis_index(axis) + 1) * x.shape[dim], axis=dim)
 
 
 def power_eight(corr):
@@ -24,7 +34,7 @@
     centered = expr - totals / samples_all
     squares = lax.psum(jnp.sum(centered * centered, axis=0), "row")
     z = (centered / jnp.sqrt(squares + 1e-06)).astype(jnp.bfloat16)
-    zcol = lax.all_gather(z, "row", axis=0, tiled=True)
+    zcol = around_the_ring(z, "row", 0)
     width = zcol.shape[1]
     slab = width // n_row
     row_id = lax.axis_index("row")

time: 336 us -> 403 us (1.20)
  local copies, waits for them, and re-layouts: 21.1 us -> 76.5 us
  waiting for transfers between devices: 173 us -> 181 us
    ppermute x0 -> x3, waiting for transfers between devices: none -> 74.5 us  [around_the_ring(): lax.ppermute(moving, axis, [(i, (i + 1) % n_dev) for i in range(n_dev)])]
    all_gather x1 -> x0, waiting for transfers between devices: 59.8 us -> none  [body(): zcol = lax.all_gather(z, 'row', axis=0, tiled=True)]
    concatenate x0 -> x1, local copies, waits for them, and re-layouts: none -> 54 us  [around_the_ring(): return jnp.roll(merged, (lax.axis_index(axis) + 1) * x.shape[dim], axis=dim)]
    dynamic_slice x0 -> x2, local copies, waits for them, and re-layouts: none -> 13.9 us  [around_the_ring(): return jnp.roll(merged, (lax.axis_index(axis) + 1) * x.shape[dim], axis=dim)]
    unnamed x6, local copies, waits for them, and re-layouts: 13.8 us -> 1.04 us
    all_gather x1, waiting for transfers between devices: 78.8 us -> 72.9 us  [body(): zrows = lax.all_gather(zpiece, 'col', axis=1, tiled=True)]
  transfers between devices with their start and end apart: 4 -> 6, of which waited for: 3 -> 5; matrix products, arithmetic and copies ran while one was open for 18% -> 16% of each run, Pallas kernels for 0% -> 0%
where the time goes in v1:
time: 403 us; the launch traced here: 400 us
  waiting for transfers between devices  181 us (45%)
  local copies, waits for them, and re-layouts  76.5 us (19%)
  matrix products  72.3 us (18%)
  blocking collectives  48.7 us (12%)
  between operations  13.8 us (3%)
  other arithmetic  5.17 us (1%)
    ppermute x3, waiting for transfers between devices, around_the_ring(): lax.ppermute(moving, axis, [(i, (i + 1) % n_dev) for i in range(n_dev)])  74.5 us
    all_gather x1, waiting for transfers between devices, body(): zrows = lax.all_gather(zpiece, 'col', axis=1, tiled=True)  72.9 us
    dot_general x2, matrix products, inner_first(): lax.dot_general(left, right, (((0,), (0,)), ((), ())), preferred_element_...  72.3 us
    concatenate x1, local copies, waits for them, and re-layouts, around_the_ring(): return jnp.roll(merged, (lax.axis_index(axis) + 1) * x.shape[dim], axis=dim)  54 us
    reduce_scatter x1, waiting for transfers between devices, body(): lax.psum_scatter(inner_first(panel, adj), 'row', scatter_dimension=0, til...  34.1 us
    psum x1, blocking collectives, body(): totals = lax.psum(jnp.sum(expr, axis=0), 'row')  17.5 us
    psum x1, blocking collectives, body(): degree = lax.psum(partial_degree, 'row')  17.3 us
    dynamic_slice x2, local copies, waits for them, and re-layouts, around_the_ring(): return jnp.roll(merged, (lax.axis_index(axis) + 1) * x.shape[dim], axis=dim)  13.9 us
  transfers between devices with their start and end apart: 6, of which 5 were waited for; matrix products, arithmetic and copies ran while one was open for 16% of the time, Pallas kernels for 0%

profile of v1, /device:TPU:0, one launch (start us, length us, event | category | flops | bytes accessed | tf_op | source)
XLA Modules:
  0.0 399.9 jit_solution(5904434342051507177)
XLA Ops:
  7.2 0.0 copy-start
  7.2 0.0 all-gather.2.cloned.1.call-start
  7.2 2.0 reduce_sum.27
  9.2 17.5 %psum.28 = f32[4096]{0:T(1024)S(1)} all-reduce(f32[4096]{0:T(1024)S(1)} %reduce_sum.27), channel_id=1, replica_groups=mesh['tissue'=2,'row'=4,'col'=4] {'row'}, use_global_device_ids=true, to_apply=%region_1.0 | all-reduce | flops 4096 | bytes 32768 | tf_op jit(solution)/shard_map/psum | solution.py:33
  26.7 2.0 multiply_reduce_fusion
  28.7 13.9 %psum.29 = f32[4096]{0:T(1024)S(1)} all-reduce(f32[4096]{0:T(1024)S(1)} %multiply_reduce_fusion), channel_id=1, replica_groups=mesh['tissue'=2,'row'=4,'col'=4] {'row'}, use_global_device_ids=true, to_apply=%region_3.0 | all-reduce | flops 4096 | bytes 32768 | tf_op jit(solution)/shard_map/psum | solution.py:35
  42.6 0.0 copy-done
  42.6 0.3 divide_convert_fusion
  42.9 1.0 copy-done.1
  43.9 1.0 collective-permute-start
  44.9 26.6 %collective-permute-done = bf16[150,4096]{1,0:T(8,128)(2,1)S(1)} collective-permute-done((bf16[150,4096]{1,0:T(8,128)(2,1)S(1)}, bf16[150,4096]{1,0:T(8,128)(2,1)S(1)}, u32[]{:S(2)}, u32[]{:S(2)}) %collective-permute-start) | collective-permute-done | bytes 1228832 | tf_op jit(solution)/shard_map/ppermute | solution.py:11
  71.5 0.3 collective-permute-start.1
  71.8 27.2 %collective-permute-done.1 = bf16[150,4096]{1,0:T(8,128)(2,1)S(1)} collective-permute-done((bf16[150,4096]{1,0:T(8,128)(2,1)S(1)}, bf16[150,4096]{1,0:T(8,128)(2,1)S(1)}, u32[]{:S(2)}, u32[]{:S(2)}) %collective-permute-start.1) | collective-permute-done | bytes 1228832 | tf_op jit(solution)/shard_map/ppermute | solution.py:11
  99.0 0.3 collective-permute-start.2
  99.3 20.7 %collective-permute-done.2 = bf16[150,4096]{1,0:T(8,128)(2,1)} collective-permute-done((bf16[150,4096]{1,0:T(8,128)(2,1)S(1)}, bf16[150,4096]{1,0:T(8,128)(2,1)}, u32[]{:S(2)}, u32[]{:S(2)}) %collective-permute-start.2) | collective-permute-done | bytes 1228832 | tf_op jit(solution)/shard_map/ppermute | solution.py:11
  120.1 54.0 %concatenate.6 = bf16[1200,4096]{1,0:T(8,128)(2,1)} concatenate(bf16[150,4096]{1,0:T(8,128)(2,1)} %collective-permute-done.2, bf16[150,4096]{1,0:T(8,128)(2,1)S(1)} %collective-permute-done.1, bf16[150,4096]{1,0:T(8,128)(2,1)S(1)} %collective-permute-done, bf16[150,4096]{1,0:T(8,128)(2,1)} %copy-done.1, bf16[150,4096]{1,0:T(8,128)(2,1)} %collective-permute-done.2, ...), dimensions={0} | concatenate | bytes 19660800 | tf_op jit(solution)/shard_map/jit(_roll_dynamic)/concatenate | solution.py:14
  174.1 3.1 dynamic_slice.7
  177.2 0.0 all-gather.2.cloned.1.call-update
  177.2 0.0 all-reduce.2.cloned.1.call-start
  177.2 0.0 copy-done.2
  177.3 6.0 %constant_dynamic-slice_fusion = bf16[600,4096]{1,0:T(8,128)(2,1)} fusion(bf16[1200,4096]{1,0:T(8,128)(2,1)} %concatenate.6, s32[]{:T(128)S(6)} %select_n.57), kind=kLoop, calls=%fused_computation.34 | loop fusion | bytes 9830404 | tf_op jit(solution)/shard_map/jit(_roll_dynamic)/dynamic_slice | solution.py:14
  183.3 7.9 %copy.13 = bf16[600,4096]{0,1:T(8,128)(2,1)} copy(bf16[600,4096]{1,0:T(8,128)(2,1)} %constant_dynamic-slice_fusion) | data formatting | bytes 9830400 | tf_op jit(solution)/shard_map/jit(_roll_dynamic)/dynamic_slice | solution.py:14
  191.2 4.5 %gather_fusion = bf16[256,600]{1,0:T(8,128)(2,1)S(1)} fusion(bf16[600,4096]{0,1:T(8,128)(2,1)} %copy.13, s32[1024]{0:T(1024)S(1)} %pad_clamp_fusion), kind=kCustom, calls=%fused_computation | custom fusion | bytes 615424 | tf_op jit(solution)/shard_map/jit(_take)/gather | solution.py:54
  195.7 0.9 select_bitcast_fusion
  196.6 0.0 all-reduce.2.cloned.1.call-update
  196.6 0.2 reduce-scatter.2.cloned.1.call-start
  196.8 72.9 %all-gather.2.cloned.1.call-done = bf16[600,4096]{1,0:T(8,128)(2,1)} async-done(((bf16[600,1024]{1,0:T(8,128)(2,1)}), bf16[600,4096]{1,0:T(8,128)(2,1)}) %all-gather.2.cloned.1.call-update) | async-done | bytes 4915216 | tf_op jit(solution)/shard_map/all_gather | solution.py:43
  269.7 45.1 %select_reduce_fusion = (f32[4096]{0:T(1024)S(1)}, bf16[4096,4096]{1,0:T(8,128)(2,1)}) fusion(s32[4096]{0:T(1024)S(1)} %get-tuple-element.8, s32[4096]{0:T(1024)S(1)} %get-tuple-element.7, bf16[600,4096]{1,0:T(8,128)(2,1)} %all-gather.2.cloned.1.call-done, bf16[600,4096]{1,0:T(8,128)(2,1)} %constant_dynamic-slice_fusion), kind=kOutput, calls=%fused_computation.1 | convolution fusion | flops 20300427264 | bytes 43433984 | tf_op jit(solution)/shard_map/dot_general | solution.py:25
  314.8 27.1 %fusion.5 = f32[256,4096]{1,0:T(8,128)} fusion(bf16[4096,4096]{1,0:T(8,128)(2,1)} %get-tuple-element.6, bf16[600,4096]{1,0:T(8,128)(2,1)} %all-gather.2.cloned.1.call-done, bf16[600,256]{0,1:T(8,128)(2,1)} %all-reduce.2.cloned.1.call-done), kind=kOutput, calls=%fused_computation.11 | convolution fusion | flops 9854517248 | bytes 42971136 | tf_op jit(solution)/shard_map/dot_general | solution.py:25
  342.0 0.0 reduce-scatter.2.cloned.1.call-update
  342.0 17.3 %psum.31 = f32[4096]{0:T(1024)} all-reduce(f32[4096]{0:T(1024)S(1)} %get-tuple-element.5), channel_id=1, replica_groups=mesh['tissue'=2,'row'=4,'col'=4] {'row'}, use_global_device_ids=true, to_apply=%region_7.8 | all-reduce | flops 4096 | bytes 32768 | tf_op jit(solution)/shard_map/psum | solution.py:50
  359.3 34.1 %reduce-scatter.2.cloned.1.call-done = f32[64,4096]{1,0:T(8,128)} async-done(((f32[256,4096]{1,0:T(8,128)}), f32[64,4096]{1,0:T(8,128)}) %reduce-scatter.2.cloned.1.call-update) | async-done | bytes 1048592 | tf_op jit(solution)/shard_map/reduce_scatter | solution.py:58
  (8 shorter events, 0.1 us)
Async XLA Ops:
  7.2 35.4 %copy-start = (f32[150,4096]{1,0:T(8,128)S(1)}, f32[150,4096]{1,0:T(8,128)}, u32[]{:S(2)}) copy-start(f32[150,4096]{1,0:T(8,128)} %param.2) | copy-start | bytes 7372804
  7.2 262.5 %all-gather.2.cloned.1.call-start = ((), (), s32[]{:S(2)}) async-start(), calls=%async_computation.1 | async-start | bytes 6144000 | tf_op jit(solution)/shard_map/all_gather | solution.py:43
  42.9 1.0 copy-start.1
  43.9 27.5 %collective-permute-start = (bf16[150,4096]{1,0:T(8,128)(2,1)S(1)}, bf16[150,4096]{1,0:T(8,128)(2,1)S(1)}, u32[]{:S(2)}, u32[]{:S(2)}) collective-permute-start(bf16[150,4096]{1,0:T(8,128)(2,1)S(1)} %divide_convert_fusion), channel_id=1, source_target_pairs={{0,4},{4,8},{8,12},{12,0},{1,5},{5,9},{9,13},{13,1},{2,6},{6,10},{... | collective-permute-start | bytes 3686408 | tf_op jit(solution)/shard_map/ppermute | solution.py:11
  71.5 27.5 %collective-permute-start.1 = (bf16[150,4096]{1,0:T(8,128)(2,1)S(1)}, bf16[150,4096]{1,0:T(8,128)(2,1)S(1)}, u32[]{:S(2)}, u32[]{:S(2)}) collective-permute-start(bf16[150,4096]{1,0:T(8,128)(2,1)S(1)} %collective-permute-done), channel_id=1, source_target_pairs={{0,4},{4,8},{8,12},{12,0},{1,5},{5,9},{9,13},{13,1},{2,6},{6,10},{... | collective-permute-start | bytes 3686408 | tf_op jit(solution)/shard_map/ppermute | solution.py:11
  99.0 21.1 %collective-permute-start.2 = (bf16[150,4096]{1,0:T(8,128)(2,1)S(1)}, bf16[150,4096]{1,0:T(8,128)(2,1)}, u32[]{:S(2)}, u32[]{:S(2)}) collective-permute-start(bf16[150,4096]{1,0:T(8,128)(2,1)S(1)} %collective-permute-done.1), channel_id=1, source_target_pairs={{0,4},{4,8},{8,12},{12,0},{1,5},{5,9},{9,13},{13,1},{2,6},{6,10},{... | collective-permute-start | bytes 3686408 | tf_op jit(solution)/shard_map/ppermute | solution.py:11
  99.3 77.9 %copy-start.2 = (s32[256]{0:T(256)S(1)}, s32[256]{0:T(256)}, u32[]{:S(2)}) copy-start(s32[256]{0:T(256)} %param.3) | copy-start | bytes 3076
  177.2 137.6 %all-reduce.2.cloned.1.call-start = ((), (), s32[]{:S(2)}) async-start(), calls=%async_computation.2 | async-start | bytes 655360 | tf_op jit(solution)/shard_map/psum | solution.py:56
  196.6 196.7 %reduce-scatter.2.cloned.1.call-start = ((), (), s32[]{:S(2)}) async-start(), calls=%async_computation.3 | async-start | bytes 5242880 | tf_op jit(solution)/shard_map/reduce_scatter | solution.py:58
Sparse Core Ops, SparseCore 0:
  177.3 92.3 all-gather.1
  272.6 34.8 all-reduce.1
  342.1 51.1 reduce-scatter.1
